TPU v7x, 128 devices: a whole 4x4x4 slice. The times are simulated.
128 devices in a mesh: dp: 1, tp2: 16 (over z, y), tp: 8 (over x, core).
Axes of the slice: x: 4, y: 4, z: 4, core: 2. Of those that a mesh axis runs over, the one named last changes fastest.
Arguments:
- attn_out: bfloat16 [32768, 4096], P('dp', 'tp')
- w_out: bfloat16 [4096, 4096], P('tp', 'tp2')
- residual: bfloat16 [32768, 4096], P(('dp', 'tp'), 'tp2')
- norm_gain: float32 [4096], P('tp2')
Outputs:
- output 1: bfloat16 [32768, 4096], P(('dp', 'tp'), 'tp2')
- output 2: bfloat16 [32768, 4096], P(('dp', 'tp'), 'tp2')
All inputs are finite; a program needn't handle non-finite values.
Results may differ from a plain program's by a relative error of at most 0.00634374.
Values are sent between devices in bfloat16 or wider.
A program may use at most 1 GiB of HBM per device.

v0:
```python
import jax
import jax.numpy as jnp
from jax import lax
from jax.sharding import PartitionSpec as P, NamedSharding

EPS_NORM = 1e-6


def solution(mesh):
    tp_size = mesh.shape["tp"]
    col_groups = mesh.shape["tp2"]

    def local_step(attn_blk, w_blk, res_blk, gain_blk):
        block_prod = jnp.dot(attn_blk, w_blk, preferred_element_type=jnp.float32).astype(jnp.bfloat16)
        token_rows, local_cols = block_prod.shape
        received = lax.all_to_all(block_prod, "tp", 0, 0, tiled=True)
        y_sum = jnp.sum(received.reshape(tp_size, token_rows // tp_size, local_cols), axis=0, dtype=jnp.float32)
        hidden = res_blk.astype(jnp.float32) + y_sum
        sq_sum = lax.psum(jnp.sum(hidden * hidden, axis=-1, keepdims=True), "tp2")
        inv_rms = lax.rsqrt(sq_sum / (local_cols * col_groups) + EPS_NORM)
        normed = hidden * inv_rms * gain_blk
        return hidden.astype(jnp.bfloat16), normed.astype(jnp.bfloat16)

    row_spec = P(("dp", "tp"), "tp2")
    return jax.shard_map(local_step, mesh=mesh, in_specs=(P("dp", "tp"), P("tp", "tp2"), row_spec, P("tp2")), out_specs=(row_spec, row_spec), check_vma=False)
```

profile of v0, /device:TPU:0, one launch (start us, length us, event | category | flops | bytes accessed | tf_op | source)
XLA Modules:
  0.0 296.6 jit_solution(9324013212943169949)
XLA Ops:
  0.6 0.0 copy-start
  0.6 0.9 copy-done
  1.6 21.0 %convolution_convert_fusion = bf16[32768,256]{1,0:T(8,128)(2,1)} fusion(bf16[32768,512]{1,0:T(8,128)(2,1)} %param.4, bf16[512,256]{1,0:T(8,128)(2,1)S(1)} %copy-done), kind=kOutput, calls=%fused_computation | convolution fusion | flops 8598323200 | bytes 50593792 | tf_op jit(solution)/shard_map/dot_general | solution.py:14
  22.5 188.8 %all_to_all.9 = bf16[8,4096,256]{2,1,0:T(8,128)(2,1)S(1)} all-to-all(bf16[8,4096,256]{2,1,0:T(8,128)(2,1)} %bitcast.5), channel_id=1, replica_groups=mesh['dp'=1,'tp2'=16,'tp'=8] {'tp'}, dimensions={0} | all-to-all | bytes 33554432 | tf_op jit(solution)/shard_map/all_to_all | solution.py:16
  211.3 0.0 copy-start.3
  211.3 2.7 convert_reduce_fusion
  214.1 0.0 copy-start.2
  214.1 1.9 copy-done.2
  216.0 0.0 copy-done.3
  216.0 0.0 copy-start.4
  216.0 0.6 multiply_reduce_fusion
  216.7 75.9 %psum.7 = f32[4096,1]{0,1:T(1,128)S(1)} all-reduce(f32[4096,1]{0,1:T(1,128)S(1)} %bitcast.7), channel_id=1, replica_groups=mesh['dp'=1,'tp2'=16,'tp'=8] {'tp2'}, use_global_device_ids=true, to_apply=%region_2.0 | all-reduce | flops 4096 | bytes 32768 | tf_op jit(solution)/shard_map/psum | solution.py:19
  292.6 0.0 copy-start.1
  292.6 0.0 copy-done.4
  292.6 4.0 %multiply_convert_fusion = (bf16[4096,256]{1,0:T(8,128)(2,1)}, bf16[4096,256]{1,0:T(8,128)(2,1)}) fusion(f32[256]{0:T(256)S(1)} %copy-done.4, f32[4096]{0:T(1024)S(1)} %bitcast.6, f32[4096,256]{1,0:T(8,128)} %copy-done.2, bf16[4096,256]{1,0:T(8,128)(2,1)S(1)} %copy-done.3), kind=kLoop, calls=%fused_computation.2 | loop fusion | flops 6291456 | bytes 10503168 | tf_op jit(solution)/shard_map/convert_element_type | solution.py:22
  296.6 0.0 copy-done.1
  (1 shorter events, 0.0 us)
Async XLA Ops:
  0.6 1.0 copy-start
  211.3 4.7 %copy-start.3 = (bf16[4096,256]{1,0:T(8,128)(2,1)S(1)}, bf16[4096,256]{1,0:T(8,128)(2,1)}, u32[]{:S(2)}) copy-start(bf16[4096,256]{1,0:T(8,128)(2,1)} %param.6) | copy-start | bytes 6291460
  214.1 1.9 copy-start.2
  216.0 76.6 %copy-start.4 = (f32[256]{0:T(256)S(1)}, f32[256]{0:T(256)}, u32[]{:S(2)}) copy-start(f32[256]{0:T(256)} %param.7) | copy-start | bytes 3076
  292.6 4.0 %copy-start.1 = (bf16[512,256]{1,0:T(8,128)(2,1)S(1)}, bf16[512,256]{1,0:T(8,128)(2,1)}, u32[]{:S(2)}) copy-start(bf16[512,256]{1,0:T(8,128)(2,1)} %param.5) | copy-start | bytes 786436
where the time goes:
time: 297 us
  blocking collectives  265 us (89%)
  matrix products  21 us (7%)
  other arithmetic  7.42 us (2%)
    all_to_all x1, blocking collectives, local_step(): received = lax.all_to_all(block_prod, 'tp', 0, 0, tiled=True)  189 us
    psum x1, blocking collectives, local_step(): sq_sum = lax.psum(jnp.sum(hidden * hidden, axis=-1, keepdims=True), 'tp2')  75.9 us
    dot_general x1, matrix products, local_step(): jnp.dot(attn_blk, w_blk, preferred_element_type=jnp.float32)  21 us

commit v1 on v0

v1 whole, which is shorter than its diff:
```python
import jax
import jax.numpy as jnp
from jax import lax
from jax.experimental import pallas as pl
from jax.experimental.pallas import tpu as pltpu
from jax.sharding import PartitionSpec as P

EPS_NORM = 1e-6
MESH = pl.DeviceIdType.MESH
BF16, F32 = jnp.bfloat16, jnp.float32

NC = 8
CR = 128
SUB = 32
KB = 512
CB = 256
WZ = 256


def kernel(a_hbm, w_hbm, r_hbm, g_ref, h_hbm, n_hbm,
           abuf, wbuf, yout, yin, rbuf, hbuf, nbuf, sq,
           l_sem, a_s, a_r, p_s, p_r, b_s, b_r, f_s, f_r, w_s, w_r, d_s, d_r, y_s, y_r, q_s, q_r, o_s):
    tp, t2 = lax.axis_index("tp"), lax.axis_index("tp2")
    x, c, z, y = tp // 2, tp % 2, t2 // 4, t2 % 4

    def dev(dx=0, dy=0, dz=0, core=None):
        return {"tp": ((x + dx) % 4) * 2 + (c if core is None else core), "tp2": ((z + dz) % 4) * 4 + (y + dy) % 4}

    def rdma(src, dst, ssem, rsem, device):
        return pltpu.make_async_remote_copy(src_ref=src, dst_ref=dst, send_sem=ssem, recv_sem=rsem,
                                            device_id=device, device_id_type=MESH)

    ym, yp = (y + 3) % 4, (y + 1) % 4

    def cross(k, d, cd):
        block = (((x + d) % 4) * 2 + cd) * (4 * NC) + z * NC + k
        return rdma(a_hbm.at[block, y], abuf.at[k, y, c, (4 - d) % 4], a_s.at[k, d - 1, cd], a_r.at[k, c],
                    dev(dx=d, core=cd))

    def cross_wait(k, cc):
        view = abuf.at[k, y, cc, pl.ds(1, 3)]
        pltpu.make_async_copy(view, view, a_r.at[k, cc]).wait()

    def bcast(k, cc, back):
        view = abuf.at[k, y, cc, pl.ds(1, 3)]
        return rdma(view, view, b_s.at[k, cc, back], b_r.at[k, cc, back], dev(dy=3 if back else 1))

    def forward(k, back):
        view = abuf.at[k, yp if back else ym, back, pl.ds(1, 3)]
        return rdma(view, view, f_s.at[k, back], f_r.at[k, back], dev(dy=3 if back else 1))

    def ysend(k, zr):
        return rdma(yout.at[k, zr - 1], yin.at[z * NC + k], y_s.at[k, zr - 1], y_r.at[k, zr - 1], dev(dz=zr))

    def wview(part, j, zr):
        return wbuf.at[j, c, zr, pl.ds(0, WZ) if part == 0 else pl.ds(WZ, KB - WZ)]

    w_sends = []

    def wsend(part, src_slot, dst_slot, device):
        n = len(w_sends)
        copy = rdma(wview(part, *src_slot), wview(part, *dst_slot), w_s.at[n],
                    w_r.at[part, dst_slot[0] * 4 + dst_slot[1]], device)
        w_sends.append(copy)
        copy.start()

    def wwait(part, slot):
        view = wview(part, *slot)
        pltpu.make_async_copy(view, view, w_r.at[part, slot[0] * 4 + slot[1]]).wait()

    def dcopy(part, slot):
        view = wview(part, *slot)
        n = slot[0] * 4 + slot[1]
        return rdma(view, view, d_s.at[part, n], d_r.at[part, n], dev(core=1 - c))

    own_a = pltpu.make_async_copy(a_hbm.at[pl.ds(tp * (4 * NC) + z * NC, NC)], abuf.at[:, :, c, 0], l_sem.at[0])
    own_w = pltpu.make_async_copy(w_hbm, wbuf.at[0, c, 0], l_sem.at[1])
    own_r = pltpu.make_async_copy(r_hbm, rbuf, l_sem.at[2])
    own_w.start()
    own_a.start()
    own_r.start()

    barrier = pltpu.get_barrier_semaphore()
    peers = [dev(dx=d, core=cd) for d in (1, 2, 3) for cd in (0, 1)] + [dev(core=1 - c)]
    peers += [dev(dy=1), dev(dy=3), dev(dz=1), dev(dz=2), dev(dz=3)]
    for peer in peers:
        pl.semaphore_signal(barrier, inc=1, device_id=peer, device_id_type=MESH)
    pl.semaphore_wait(barrier, len(peers))

    def cross_start(k):
        for d in (1, 3, 2):
            for cd in (0, 1):
                cross(k, d, cd).start()

    partner_a = rdma(a_hbm.at[pl.ds((tp + 1 - 2 * c) * (4 * NC) + z * NC, NC)], abuf.at[:, :, c, 0],
                     p_s, p_r, dev(core=1 - c))
    cross_start(0)
    own_w.wait()
    for zr, dz in ((3, 1), (1, 3), (2, 2)):
        wsend(0, (0, 0), (0, zr), dev(dz=dz))
    for j, dx in ((3, 1), (1, 3), (2, 2)):
        wsend(1, (0, 0), (j, 0), dev(dx=dx))
    cross_start(1)
    partner_a.start()
    dcopy(0, (0, 0)).start()
    dcopy(1, (0, 0)).start()

    def bcast_start(k):
        for cc in (0, 1):
            cross_wait(k, cc)
        for i in (0, 1):
            bcast(k, i, 0).start()
            bcast(k, 1 - i, 1).start()

    def forward_start(k):
        for back in (0, 1):
            bcast(k, back, back).wait_recv()
            forward(k, back).start()

    bcast_start(0)

    for zr in (3, 1, 2, 0):
        if zr:
            wwait(0, (0, zr))
            dcopy(0, (0, zr)).start()
        wsend(0, (0, zr), (3, zr), dev(dx=1))
        wsend(0, (0, zr), (1, zr), dev(dx=3))
    for j in (0, 3, 1, 2):
        if j:
            wwait(1, (j, 0))
            dcopy(1, (j, 0)).start()
        wsend(1, (j, 0), (j, 3), dev(dz=1))
        wsend(1, (j, 0), (j, 1), dev(dz=3))
    cross_start(2)
    bcast_start(1)
    forward_start(0)

    for i in (0, 1):
        for j, zr, dx in ((3, (3, 1)[i], 1), (1, (2, 0)[i], 3)):
            wwait(0, (j, zr))
            wsend(0, (j, zr), (2, zr), dev(dx=dx))
            dcopy(0, (j, zr)).start()
        for zr, j, dz in ((3, (0, 3)[i], 1), (1, (1, 2)[i], 3)):
            wwait(1, (j, zr))
            wsend(1, (j, zr), (j, 2), dev(dz=dz))
            dcopy(1, (j, zr)).start()
    for k in range(3, NC):
        cross_start(k)
    for slot in ((3, 2), (3, 0), (1, 3), (1, 1)):
        wwait(0, slot)
        dcopy(0, slot).start()
    for slot in ((1, 3), (2, 3), (0, 1), (3, 1)):
        wwait(1, slot)
        dcopy(1, slot).start()
    for n in range(4):
        wwait(0, (2, n))
        dcopy(0, (2, n)).start()
        wwait(1, (n, 2))
        dcopy(1, (n, 2)).start()
    own_a.wait()
    partner_a.wait_recv()
    for n in range(16):
        for part in (0, 1):
            dcopy(part, (n // 4, n % 4)).wait_recv()

    def tile(k, zr, out):
        for j in range(4):
            for cc in (0, 1):
                lhs = abuf[k, :, cc, j].reshape(CR, KB)
                term = jnp.dot(lhs, wbuf[j, cc, zr], preferred_element_type=F32).astype(BF16).astype(F32)
                if j == 0 and cc == 0:
                    out[...] = term
                else:
                    out[...] += term

    def step(k, carry):
        @pl.when(k < NC - 2)
        def _():
            bcast_start(k + 2)

        @pl.when(k < NC - 1)
        def _():
            forward_start(k + 1)

        for back in (0, 1):
            bcast(k, 1 - back, back).wait_recv()
            forward(k, back).wait_recv()
        for zr in (1, 3, 2):
            tile(k, zr, yout.at[k, zr - 1])
            ysend(k, zr).start()
        tile(k, 0, yin.at[z * NC + k])
        return carry

    lax.fori_loop(0, NC, step, 0)

    own_r.wait()

    def qsend(g, n):
        view = sq.at[g, t2]
        return rdma(view, view, q_s.at[g, n - 1], q_r.at[g], dev(dy=n % 4, dz=n // 4))

    def square_group(g):
        for i in (0, 1):
            k = 2 * g + i
            for zr in (1, 2, 3):
                ysend(k, zr).wait_recv()
            for q in range(4):
                hid = yin[q * NC + k] + rbuf[q, pl.ds(k * CR, CR), :].astype(F32)
                yin[q * NC + k] = hid
                hbuf[q, pl.ds(k * CR, CR), :] = hid.astype(BF16)
                total = jnp.sum(hid * hid, axis=1, keepdims=True)
                sq[g, t2, pl.ds(i * 4 + q, 1), :] = jnp.broadcast_to(total, (CR, 128)).T[0:1, :]
        for n in range(1, 16):
            qsend(g, n).start()
        out_copy(hbuf, h_hbm, g, 0).start()

    def out_copy(buf, dst, g, which):
        rows = pl.ds(g * (2 * CR), 2 * CR)
        return pltpu.make_async_copy(buf.at[:, rows], dst.at[:, rows], o_s.at[g, which])

    def norm_group(g):
        view = sq.at[g, pl.ds(0, 15)]
        pltpu.make_async_copy(view, view, q_r.at[g]).wait()
        inv = lax.rsqrt(jnp.sum(sq[g], axis=0) * (1.0 / 4096) + EPS_NORM)
        for i in (0, 1):
            k = 2 * g + i
            for q in range(4):
                scale = jnp.broadcast_to(inv[i * 4 + q:i * 4 + q + 1, :], (128, CR)).T
                for half in (0, 1):
                    cols = pl.ds(half * 128, 128)
                    nbuf[q, pl.ds(k * CR, CR), cols] = (
                        yin[q * NC + k, :, cols] * scale * g_ref[:, cols]).astype(BF16)
        out_copy(nbuf, n_hbm, g, 1).start()

    groups = NC // 2

    def finish(g, carry):
        @pl.when(g < groups)
        def _():
            square_group(g)

        @pl.when(g >= 1)
        def _():
            norm_group(g - 1)

        return carry

    lax.fori_loop(0, groups + 1, finish, 0)

    for copy in w_sends:
        copy.wait_send()
    partner_a.wait_send()
    for n in range(16):
        for part in (0, 1):
            dcopy(part, (n // 4, n % 4)).wait_send()

    def drain(k, carry):
        for d in (1, 2, 3):
            for cd in (0, 1):
                cross(k, d, cd).wait_send()
            ysend(k, d).wait_send()
        for back in (0, 1):
            bcast(k, 0, back).wait_send()
            bcast(k, 1, back).wait_send()
            forward(k, back).wait_send()
        return carry

    lax.fori_loop(0, NC, drain, 0)

    def drain_group(g, carry):
        for n in range(1, 16):
            qsend(g, n).wait_send()
        out_copy(hbuf, h_hbm, g, 0).wait()
        out_copy(nbuf, n_hbm, g, 1).wait()
        return carry

    lax.fori_loop(0, groups, drain_group, 0)


def solution(mesh):
    def local_step(attn_blk, w_blk, res_blk, gain_blk):
        any_spec = pl.BlockSpec(memory_space=pl.ANY)
        out = jax.ShapeDtypeStruct((4, NC * CR, CB), BF16)
        dma = pltpu.SemaphoreType.DMA
        h, n = pl.pallas_call(
            kernel,
            out_shape=(out, out),
            in_specs=[any_spec, any_spec, any_spec, pl.BlockSpec(memory_space=pltpu.VMEM)],
            out_specs=(any_spec, any_spec),
            scratch_shapes=[
                pltpu.VMEM((NC, 4, 2, 4, SUB, KB), BF16),
                pltpu.VMEM((4, 2, 4, KB, CB), BF16),
                pltpu.VMEM((NC, 3, CR, CB), F32),
                pltpu.VMEM((4 * NC, CR, CB), F32),
                pltpu.VMEM((4, NC * CR, CB), BF16),
                pltpu.VMEM((4, NC * CR, CB), BF16),
                pltpu.VMEM((4, NC * CR, CB), BF16),
                pltpu.VMEM((NC // 2, 16, 8, 128), F32),
                dma((3,)),
                dma((NC, 3, 2)), dma((NC, 2)),
                dma, dma,
                dma((NC, 2, 2)), dma((NC, 2, 2)),
                dma((NC, 2)), dma((NC, 2)),
                dma((30,)), dma((2, 16)),
                dma((2, 16)), dma((2, 16)),
                dma((NC, 3)), dma((NC, 3)),
                dma((NC // 2, 15)), dma((NC // 2,)),
                dma((NC // 2, 2)),
            ],
            compiler_params=pltpu.CompilerParams(
                collective_id=0, has_side_effects=True, vmem_limit_bytes=60 * 1024 * 1024),
        )(attn_blk.reshape(8 * 4 * NC, 4, SUB, KB), w_blk, res_blk.reshape(4, NC * CR, CB), gain_blk.reshape(1, CB))
        return h.reshape(4 * NC * CR, CB), n.reshape(4 * NC * CR, CB)

    row_spec = P(("dp", "tp"), "tp2")
    return jax.shard_map(local_step, mesh=mesh, in_specs=(P("dp", "tp"), P("tp", "tp2"), row_spec, P("tp2")),
                         out_specs=(row_spec, row_spec), check_vma=False)
```

time: 297 us -> 114 us (0.38)
  blocking collectives: 265 us -> 0 us
  Pallas kernels: 0 us -> 108 us
  matrix products: 21 us -> 0 us
  other arithmetic: 7.42 us -> 0 us
    all_to_all x1 -> x0, blocking collectives: 189 us -> none  [local_step(): received = lax.all_to_all(block_prod, 'tp', 0, 0, tiled=True)]
    pallas_call x0 -> x1, Pallas kernels: none -> 108 us  [local_step(): pl.pallas_call(kernel, out_shape=(out, out), in_specs=[any_spec, any_spec...]
    psum x1 -> x0, blocking collectives: 75.9 us -> none  [local_step(): sq_sum = lax.psum(jnp.sum(hidden * hidden, axis=-1, keepdims=True), 'tp2')]
    dot_general x1 -> x0, matrix products: 21 us -> none  [local_step(): jnp.dot(attn_blk, w_blk, preferred_element_type=jnp.float32)]
    convert_element_type x1 -> x0, other arithmetic: 4.02 us -> none  [local_step(): return (hidden.astype(jnp.bfloat16), normed.astype(jnp.bfloat16))]
    reduce_sum x2 -> x0, other arithmetic: 3.37 us -> none  [the longest x1 2.75 us: local_step(): jnp.sum(received.reshape(tp_size, token_rows // tp_size, local_cols), axi...]
where the time goes in v1:
time: 114 us; the launch traced here: 113 us
  Pallas kernels  108 us (95%)
  local copies, waits for them, and re-layouts  4.52 us (4%)
    pallas_call x1, Pallas kernels, local_step(): pl.pallas_call(kernel, out_shape=(out, out), in_specs=[any_spec, any_spec...  108 us
    unnamed x4, local copies, waits for them, and re-layouts  4.52 us

profile of v1, /device:TPU:0, one launch (start us, length us, event | category | flops | bytes accessed | tf_op | source)
XLA Modules:
  0.0 113.3 jit_solution(18005176992603287512)
XLA Ops:
  0.6 108.1 %shard_map.59 = (bf16[4,1024,256]{2,1,0:T(8,128)(2,1)}, bf16[4,1024,256]{2,1,0:T(8,128)(2,1)}) custom-call(bf16[256,4,32,512]{3,2,1,0:T(8,128)(2,1)} %bitcast.5, bf16[512,256]{1,0:T(8,128)(2,1)} %w_hbm.1, bf16[4,1024,256]{2,1,0:T(8,128)(2,1)} %bitcast.8, f32[1,256]{1,0:T(1,128)} %bitcast.9), custom_call_target="tpu_custom_call" | custom-call | tf_op jit(solution)/shard_map/pallas_call | solution.py:285
  108.8 0.0 copy-start
  108.8 3.2 %copy.8 = bf16[4096,256]{1,0:T(8,128)(2,1)} copy(bf16[4096,256]{1,0:T(8,128)(2,1)} %bitcast.7) | data formatting | bytes 4194304
  112.0 0.0 copy-done
  112.0 1.3 %copy.9 = bf16[4096,256]{1,0:T(8,128)(2,1)} copy(bf16[4096,256]{1,0:T(8,128)(2,1)S(1)} %bitcast.6) | data formatting | bytes 4194304
Async XLA Ops:
  108.8 3.2 %copy-start = (bf16[4,1024,256]{2,1,0:T(8,128)(2,1)S(1)}, bf16[4,1024,256]{2,1,0:T(8,128)(2,1)}, u32[]{:S(2)}) copy-start(bf16[4,1024,256]{2,1,0:T(8,128)(2,1)} %get-tuple-element.5) | copy-start | bytes 6291460

commit v2 on v0

v2 whole, which is shorter than its diff:
```python
import jax
import jax.numpy as jnp
from jax import lax
from jax.experimental import pallas as pl
from jax.experimental.pallas import tpu as pltpu
from jax.sharding import PartitionSpec as P

EPS_NORM = 1e-6
MESH = pl.DeviceIdType.MESH
AROUND = (1, 3, 2)
CORES = (0, 1)
BF16, F32 = jnp.bfloat16, jnp.float32

NC = 8
NK = 7
CR = 128
SUB = 32
KB = 512
CB = 256
WZ = 256


def kernel(a_hbm, w_hbm, r_hbm, yin, inv_ref,
           abuf, wbuf, yout, rbuf, sq, ea, eout, ein,
           l_sem, a_s, a_r, p_s, p_r, b_s, b_r, f_s, f_r, w_s, w_r, d_s, d_r, y_s, y_r, q_s, q_r, e_s, e_r):
    tp, t2 = lax.axis_index("tp"), lax.axis_index("tp2")
    x, c, z, y = tp // 2, tp % 2, t2 // 4, t2 % 4

    def dev(dx=0, dy=0, dz=0, core=None):
        return {"tp": ((x + dx) % 4) * 2 + (c if core is None else core), "tp2": ((z + dz) % 4) * 4 + (y + dy) % 4}

    def rdma(src, dst, ssem, rsem, device):
        return pltpu.make_async_remote_copy(src_ref=src, dst_ref=dst, send_sem=ssem, recv_sem=rsem,
                                            device_id=device, device_id_type=MESH)

    ym, yp = (y + 3) % 4, (y + 1) % 4

    def cross(k, d, cd):
        return rdma(a_hbm.at[(((x + d) % 4) * 2 + cd) * 4 + z, k, y], abuf.at[k, y, c, (4 - d) % 4], a_s.at[k, d - 1, cd], a_r.at[k, c],
                    dev(dx=d, core=cd))

    def cross_wait(k, cc):
        view = abuf.at[k, y, cc, pl.ds(1, 3)]
        pltpu.make_async_copy(view, view, a_r.at[k, cc]).wait()

    def bcast(k, cc, back):
        view = abuf.at[k, y, cc, pl.ds(1, 3)]
        return rdma(view, view, b_s.at[k, cc, back], b_r.at[k, cc, back], dev(dy=3 if back else 1))

    def forward(k, back):
        view = abuf.at[k, yp if back else ym, back, pl.ds(1, 3)]
        return rdma(view, view, f_s.at[k, back], f_r.at[k, back], dev(dy=3 if back else 1))

    def ysend(k, zr):
        return rdma(yout.at[k, zr - 1], yin.at[z * NC + k], y_s.at[k, zr - 1], y_r.at[k, zr - 1], dev(dz=zr))

    def wview(part, j, zr):
        return wbuf.at[j, c, zr, pl.ds(0, WZ) if part == 0 else pl.ds(WZ, KB - WZ)]

    w_sent = []

    def wcopy(n, part, src_slot, dst_slot, device):
        return rdma(wview(part, *src_slot), wview(part, *dst_slot), w_s.at[n],
                    w_r.at[part, dst_slot[0] * 4 + dst_slot[1]], device)

    def wsend(part, src_slot, dst_slot, device):
        wcopy(len(w_sent), part, src_slot, dst_slot, device).start()
        w_sent.append(part)

    def wwait(part, slot):
        view = wview(part, *slot)
        pltpu.make_async_copy(view, view, w_r.at[part, slot[0] * 4 + slot[1]]).wait()

    def dcopy(part, slot):
        view = wview(part, *slot)
        n = slot[0] * 4 + slot[1]
        return rdma(view, view, d_s.at[part, n], d_r.at[part, n], dev(core=1 - c))

    own_a = pltpu.make_async_copy(a_hbm.at[tp * 4 + z, pl.ds(0, NK)], abuf.at[:, :, c, 0], l_sem.at[0])
    ex_a = pltpu.make_async_copy(a_hbm.at[:, NK], ea, l_sem.at[3])
    own_w = pltpu.make_async_copy(w_hbm, wbuf.at[0, c, 0], l_sem.at[1])
    own_r = pltpu.make_async_copy(r_hbm, rbuf, l_sem.at[2])
    own_w.start()
    ex_a.start()
    own_a.start()
    own_r.start()

    barrier = pltpu.get_barrier_semaphore()
    peers = [dev(dx=d, core=cd) for d in AROUND for cd in CORES] + [dev(core=1 - c)]
    peers += [dev(dy=1), dev(dy=3), dev(dz=1), dev(dz=2), dev(dz=3)]
    for peer in peers:
        pl.semaphore_signal(barrier, inc=1, device_id=peer, device_id_type=MESH)
    pl.semaphore_wait(barrier, len(peers))

    def cross_start(k):
        for d in AROUND:
            for cd in CORES:
                cross(k, d, cd).start()

    def bcast_start(k):
        for cc in CORES:
            cross_wait(k, cc)
        for i in CORES:
            bcast(k, i, 0).start()
            bcast(k, 1 - i, 1).start()

    def forward_start(k):
        for back in CORES:
            bcast(k, back, back).wait_recv()
            forward(k, back).start()

    def take(part, j, zr):
        wwait(part, (j, zr))
        dcopy(part, (j, zr)).start()

    def relay_x(part, j, zr):
        take(part, j, zr)
        wsend(part, (j, zr), (2, zr), dev(dx=4 - j))

    def relay_z(j, zr):
        take(1, j, zr)
        wsend(1, (j, zr), (j, 2), dev(dz=4 - zr))

    def both_x(part, zr):
        wsend(part, (0, zr), (3, zr), dev(dx=1))
        wsend(part, (0, zr), (1, zr), dev(dx=3))

    def both_z(part, j):
        wsend(part, (j, 0), (j, 3), dev(dz=1))
        wsend(part, (j, 0), (j, 1), dev(dz=3))

    partner_a = rdma(a_hbm.at[(tp + 1 - 2 * c) * 4 + z, pl.ds(0, NK)], abuf.at[:, :, c, 0],
                     p_s, p_r, dev(core=1 - c))
    own_w.wait()
    wsend(0, (0, 0), (0, 3), dev(dz=1))
    wsend(0, (0, 0), (0, 1), dev(dz=3))
    cross_start(0)
    both_z(1, 0)
    both_x(1, 0)
    wsend(1, (0, 0), (2, 0), dev(dx=2))
    wsend(0, (0, 0), (0, 2), dev(dz=2))
    cross_start(1)
    cross_start(2)
    partner_a.start()
    dcopy(0, (0, 0)).start()
    dcopy(1, (0, 0)).start()

    ex_a.wait()

    def ex_copy(d, cd):
        owner = ((x + d) % 4) * 2 + cd
        return rdma(eout.at[owner], ein.at[tp], e_s.at[d, cd], e_r.at[tp], dev(dx=d, core=cd))

    def ex_product(i, carry):
        lhs = ea[pl.ds(i * 4, 4)].reshape(4 * CR, KB)
        prod = jnp.dot(lhs, wbuf[0, c, 0], preferred_element_type=F32)
        eout[i] = prod.astype(BF16).reshape(4, CR, CB)
        return carry

    lax.fori_loop(0, 8, ex_product, 0)

    take(0, 0, 3)
    take(0, 0, 1)
    wsend(0, (0, 3), (3, 3), dev(dx=1))
    wsend(0, (0, 1), (1, 1), dev(dx=3))
    wsend(0, (0, 1), (3, 1), dev(dx=1))
    wsend(0, (0, 3), (1, 3), dev(dx=3))
    bcast_start(0)
    for j in (3, 1, 2):
        take(1, j, 0)
        both_z(1, j)
    forward_start(0)
    relay_z(0, 3)
    take(1, 0, 1)
    take(0, 0, 2)
    bcast_start(1)
    bcast_start(2)
    relay_z(1, 1)
    relay_z(3, 3)
    forward_start(1)
    relay_x(0, 3, 3)
    relay_x(0, 1, 1)
    cross_start(3)
    both_x(0, 2)
    cross_start(4)
    relay_z(2, 1)
    for slot in ((3, 1), (1, 3), (2, 3)):
        take(1, *slot)
    take(0, 3, 1)
    take(0, 1, 3)
    take(0, 2, 3)
    take(0, 2, 1)
    own_a.wait()
    partner_a.wait_recv()

    def partner_w(zr):
        for j in range(4):
            for part in CORES:
                dcopy(part, (j, zr)).wait_recv()

    partner_w(1)
    partner_w(3)

    def tile(k, zr, out):
        for j in range(4):
            for cc in CORES:
                lhs = abuf[k, :, cc, j].reshape(CR, KB)
                term = jnp.dot(lhs, wbuf[j, cc, zr], preferred_element_type=F32).astype(BF16).astype(F32)
                if j == 0 and cc == 0:
                    out[...] = term
                else:
                    out[...] += term

    def qsend(g, n):
        view = sq.at[g, t2]
        return rdma(view, view, q_s.at[g, n - 1], q_r.at[g], dev(dy=n % 4, dz=n // 4))

    def square_group(g):
        for i in CORES:
            k = 2 * g + i
            if k < NK:
                for zr in AROUND:
                    ysend(k, zr).wait_recv()
            for q in range(4):
                hid = yin[q * NC + k] + rbuf[q, pl.ds(k * CR, CR), :].astype(F32)
                yin[q * NC + k] = hid
                total = jnp.sum(hid * hid, axis=1, keepdims=True)
                sq[g, t2, pl.ds(i * 4 + q, 1), :] = jnp.broadcast_to(total, (CR, 128)).T[0:1, :]
        for n in range(1, 16):
            qsend(g, n).start()

    def norm_group(g):
        view = sq.at[g, pl.ds(0, 15)]
        pltpu.make_async_copy(view, view, q_r.at[g]).wait()
        inv_ref[g] = lax.rsqrt(jnp.sum(sq[g], axis=0) * (1.0 / 4096) + EPS_NORM)

    def step(k, carry):
        for back in CORES:
            bcast(k, 1 - back, back).wait_recv()
            forward(k, back).wait_recv()
        for zr in (1, 3):
            tile(k, zr, yout.at[k, zr - 1])
            ysend(k, zr).start()

        @pl.when(k == 0)
        def _():
            forward_start(2)
            bcast_start(3)

        @pl.when(k == 1)
        def _():
            relay_x(0, 3, 2)
            for n in range(5, NK):
                cross_start(n)
            both_x(0, 0)
            take(0, 1, 2)
            for j in range(4):
                take(1, j, 2)

        @pl.when(k == 2)
        def _():
            forward_start(3)
            bcast_start(4)
            take(0, 2, 2)
            partner_w(2)
            bcast_start(5)

        @pl.when(k == 3)
        def _():
            forward_start(4)
            bcast_start(6)
            ex_copy(0, 1 - c).start()
            for d in AROUND:
                ex_copy(d, 0).start()

        @pl.when(k == 4)
        def _():
            forward_start(5)

        def far(i, carry):
            tile(i, 2, yout.at[i, 1])
            ysend(i, 2).start()
            return carry

        lax.fori_loop(jnp.where(k == 2, 0, k), jnp.where(k < 2, 0, k + 1), far, 0)

        @pl.when(k == 4)
        def _():
            relay_x(0, 3, 0)
            take(0, 1, 0)
            for d in AROUND:
                ex_copy(d, 1).start()
            forward_start(6)

        return carry

    own_r.wait()
    lax.fori_loop(0, NK, step, 0)
    take(0, 2, 0)
    partner_w(0)

    def near(i, carry):
        tile(i, 0, yin.at[z * NC + i])
        return carry

    lax.fori_loop(0, NK, near, 0)

    def ex_arrival(i):
        return pltpu.make_async_copy(ein.at[i], ein.at[i], e_r.at[i])

    for i in range(8):
        @pl.when(tp != i)
        def _():
            ex_arrival(i).wait()

    def ex_sum(q, carry):
        total = eout[tp, q].astype(F32)
        for d in range(1, 8):
            total += ein[(tp + d) % 8, q].astype(F32)
        yin[q * NC + NK] = total
        return carry

    lax.fori_loop(0, 4, ex_sum, 0)
    for g in range(NC // 2):
        square_group(g)
    for g in range(NC // 2):
        norm_group(g)

    for n, part in enumerate(w_sent):
        wcopy(n, part, (0, 0), (1, 0), dev(dx=1)).wait_send()
    partner_a.wait_send()
    for n in range(16):
        for part in CORES:
            dcopy(part, (n // 4, n % 4)).wait_send()

    def drain(k, carry):
        for d in AROUND:
            for cd in CORES:
                cross(k, d, cd).wait_send()
            ysend(k, d).wait_send()
        for back in CORES:
            bcast(k, 0, back).wait_send()
            bcast(k, 1, back).wait_send()
            forward(k, back).wait_send()
        return carry

    lax.fori_loop(0, NK, drain, 0)
    ex_copy(0, 1 - c).wait_send()
    for d in AROUND:
        ex_copy(d, 0).wait_send()
        ex_copy(d, 1).wait_send()

    def drain_group(g, carry):
        for n in range(1, 16):
            qsend(g, n).wait_send()
        return carry

    lax.fori_loop(0, NC // 2, drain_group, 0)


def norm_kernel(yin, inv_ref, g_ref, h_hbm, n_hbm, hbuf, nbuf, sem):
    def out_copy(k, which):
        rows = pl.ds(k * CR, CR)
        buf, dst = ((hbuf, h_hbm), (nbuf, n_hbm))[which]
        return pltpu.make_async_copy(buf.at[:, rows], dst.at[:, rows], sem.at[k, which])

    def chunk(k, carry):
        rows = pl.ds(k * CR, CR)
        for q in range(4):
            inv = inv_ref[k // 2, pl.ds((k % 2) * 4 + q, 1), :]
            scale = jnp.broadcast_to(inv, (128, CR)).T
            hid = yin[q * NC + k]
            hbuf[q, rows, :] = hid.astype(BF16)
            for half in CORES:
                cols = slice(half * 128, half * 128 + 128)
                nbuf[q, rows, cols] = (hid[:, cols] * scale * g_ref[:, cols]).astype(BF16)
        out_copy(k, 0).start()
        out_copy(k, 1).start()
        return carry

    lax.fori_loop(0, NC, chunk, 0)

    def drain(k, carry):
        out_copy(k, 0).wait()
        out_copy(k, 1).wait()
        return carry

    lax.fori_loop(0, NC, drain, 0)


def solution(mesh):
    def local_step(attn_blk, w_blk, res_blk, gain_blk):
        any_spec = pl.BlockSpec(memory_space=pl.ANY)
        out = jax.ShapeDtypeStruct((4, NC * CR, CB), BF16)
        vmem_spec = pl.BlockSpec(memory_space=pltpu.VMEM)
        dma = pltpu.SemaphoreType.DMA
        hidden, inv = pl.pallas_call(
            kernel,
            out_shape=(pltpu.VMEM((4 * NC, CR, CB), F32), pltpu.VMEM((NC // 2, 8, 128), F32)),
            in_specs=[any_spec, any_spec, any_spec],
            out_specs=(vmem_spec, vmem_spec),
            scratch_shapes=[
                pltpu.VMEM((NK, 4, 2, 4, SUB, KB), BF16),
                pltpu.VMEM((4, 2, 4, KB, CB), BF16),
                pltpu.VMEM((NK, 3, CR, CB), F32),
                pltpu.VMEM((4, NC * CR, CB), BF16),
                pltpu.VMEM((NC // 2, 16, 8, 128), F32),
                pltpu.VMEM((32, 4, SUB, KB), BF16),
                pltpu.VMEM((8, 4, CR, CB), BF16),
                pltpu.VMEM((8, 4, CR, CB), BF16),
                dma((4,)),
                dma((NK, 3, 2)), dma((NK, 2)),
                dma, dma,
                dma((NK, 2, 2)), dma((NK, 2, 2)),
                dma((NK, 2)), dma((NK, 2)),
                dma((30,)), dma((2, 16)),
                dma((2, 16)), dma((2, 16)),
                dma((NK, 3)), dma((NK, 3)),
                dma((NC // 2, 15)), dma((NC // 2,)),
                dma((4, 2)), dma((8,)),
            ],
            compiler_params=pltpu.CompilerParams(
                collective_id=0, has_side_effects=True, vmem_limit_bytes=50 * 1024 * 1024),
        )(attn_blk.reshape(8 * 4, NC, 4, SUB, KB), w_blk, res_blk.reshape(4, NC * CR, CB))
        h, n = pl.pallas_call(
            norm_kernel,
            out_shape=(out, out),
            in_specs=[vmem_spec] * 3,
            out_specs=(any_spec, any_spec),
            scratch_shapes=[pltpu.VMEM((4, NC * CR, CB), BF16)] * 2 + [dma((NC, 2))],
            compiler_params=pltpu.CompilerParams(vmem_limit_bytes=12 * 1024 * 1024),
        )(hidden, inv, gain_blk.reshape(1, CB))
        return h.reshape(4 * NC * CR, CB), n.reshape(4 * NC * CR, CB)

    row_spec = P(("dp", "tp"), "tp2")
    return jax.shard_map(local_step, mesh=mesh, in_specs=(P("dp", "tp"), P("tp", "tp2"), row_spec, P("tp2")),
                         out_specs=(row_spec, row_spec), check_vma=False)
```

time: 297 us -> 95.3 us (0.32)
  blocking collectives: 265 us -> 0 us
  Pallas kernels: 0 us -> 94.4 us
  matrix products: 21 us -> 0 us
  other arithmetic: 7.42 us -> 0 us
    all_to_all x1 -> x0, blocking collectives: 189 us -> none  [local_step(): received = lax.all_to_all(block_prod, 'tp', 0, 0, tiled=True)]
    pallas_call x0 -> x2, Pallas kernels: none -> 94.4 us  [the longest x1 92.2 us: local_step(): pl.pallas_call(kernel, out_shape=(pltpu.VMEM((4 * NC, CR, CB), F32), pltp...]
    psum x1 -> x0, blocking collectives: 75.9 us -> none  [local_step(): sq_sum = lax.psum(jnp.sum(hidden * hidden, axis=-1, keepdims=True), 'tp2')]
    dot_general x1 -> x0, matrix products: 21 us -> none  [local_step(): jnp.dot(attn_blk, w_blk, preferred_element_type=jnp.float32)]
    convert_element_type x1 -> x0, other arithmetic: 4.02 us -> none  [local_step(): return (hidden.astype(jnp.bfloat16), normed.astype(jnp.bfloat16))]
    reduce_sum x2 -> x0, other arithmetic: 3.37 us -> none  [the longest x1 2.75 us: local_step(): jnp.sum(received.reshape(tp_size, token_rows // tp_size, local_cols), axi...]
where the time goes in v2:
time: 95.3 us; the launch traced here: 95.1 us
  Pallas kernels  94.4 us (99%)
    pallas_call x1, Pallas kernels, local_step(): pl.pallas_call(kernel, out_shape=(pltpu.VMEM((4 * NC, CR, CB), F32), pltp...  92.2 us
    pallas_call x1, Pallas kernels, local_step(): pl.pallas_call(norm_kernel, out_shape=(out, out), in_specs=[vmem_spec] *...  2.21 us

profile of v2, /device:TPU:0, one launch (start us, length us, event | category | flops | bytes accessed | tf_op | source)
XLA Modules:
  0.0 95.1 jit_solution(9641791359246866637)
XLA Ops:
  0.6 0.0 copy-start
  0.6 92.2 %shard_map.59 = (f32[32,128,256]{2,1,0:T(8,128)S(1)}, f32[4,8,128]{2,1,0:T(8,128)S(1)}) custom-call(bf16[32,8,4,32,512]{4,3,2,1,0:T(8,128)(2,1)} %bitcast.6, bf16[512,256]{1,0:T(8,128)(2,1)} %w_hbm.1, bf16[4,1024,256]{2,1,0:T(8,128)(2,1)} %bitcast.7), custom_call_target="tpu_custom_call" | custom-call | tf_op jit(solution)/shard_map/pallas_call | solution.py:397
  92.9 0.0 copy-done
  92.9 2.2 %shard_map.60 = (bf16[4,1024,256]{2,1,0:T(8,128)(2,1)}, bf16[4,1024,256]{2,1,0:T(8,128)(2,1)}) custom-call(f32[32,128,256]{2,1,0:T(8,128)S(1)} %get-tuple-element.6.yin, f32[4,8,128]{2,1,0:T(8,128)S(1)} %get-tuple-element.7.inv_ref, f32[1,256]{1,0:T(1,128)S(1)} %bitcast.5), custom_call_target="tpu_custom_call" | custom-call | tf_op jit(solution)/shard_map/pallas_call | solution.py:425
Async XLA Ops:
  0.6 92.2 %copy-start = (f32[256]{0:T(256)S(1)}, f32[256]{0:T(256)}, u32[]{:S(2)}) copy-start(f32[256]{0:T(256)} %param.7) | copy-start | bytes 3076

commit v3 on v2

v3 whole, which is shorter than its diff:
```python
import jax
import jax.numpy as jnp
from jax import lax
from jax.experimental import pallas as pl
from jax.experimental.pallas import tpu as pltpu
from jax.sharding import PartitionSpec as P

EPS_NORM = 1e-6
MESH = pl.DeviceIdType.MESH
AROUND = (1, 3, 2)
CORES = (0, 1)
BF16, F32 = jnp.bfloat16, jnp.float32

NC = 8
NK = 7
CR = 128
LAST = NC // 2 - 1
SUB = 32
KB = 512
CB = 256
PARTS = ((0, 256), (256, 256), (256, 128), (384, 128))
HALVES = {3: 2, 1: 3}


def kernel(a_hbm, w_hbm, r_hbm, yin, inv_ref,
           abuf, wbuf, yout, rbuf, sq, sz, ea, eout, ein,
           l_sem, a_s, a_r, p_s, p_r, b_r, f_r, w_s, w_r, d_s, d_r, y_s, y_r, q_s, q_r, e_s, e_r, z_r):
    tp, t2 = lax.axis_index("tp"), lax.axis_index("tp2")
    x, c, z, y = tp // 2, tp % 2, t2 // 4, t2 % 4

    def dev(dx=0, dy=0, dz=0, core=None):
        return {"tp": ((x + dx) % 4) * 2 + (c if core is None else core), "tp2": ((z + dz) % 4) * 4 + (y + dy) % 4}

    def rdma(src, dst, ssem, rsem, device):
        return pltpu.make_async_remote_copy(src_ref=src, dst_ref=dst, send_sem=ssem, recv_sem=rsem,
                                            device_id=device, device_id_type=MESH)

    def await_bytes(view, sem):
        pltpu.make_async_copy(view, view, sem).wait()

    ym, yp = (y + 3) % 4, (y + 1) % 4

    def cross(k, d, cd):
        return rdma(a_hbm.at[(((x + d) % 4) * 2 + cd) * 4 + z, k, y], abuf.at[k, y, c, (4 - d) % 4], a_s, a_r.at[k],
                    dev(dx=d, core=cd))

    def bcast(k, cc, back):
        view = abuf.at[k, y, cc, pl.ds(1, 3)]
        return rdma(view, view, a_s, b_r.at[k, back] if cc == back else f_r.at[k], dev(dy=3 if back else 1))

    def forward(k, back):
        view = abuf.at[k, yp if back else ym, back, pl.ds(1, 3)]
        return rdma(view, view, a_s, f_r.at[k], dev(dy=3 if back else 1))

    def ysend(k, zr):
        return rdma(yout.at[k, zr - 1], yin.at[z * NC + k], y_s, y_r.at[k], dev(dz=zr))

    def wview(part, j, zr):
        return wbuf.at[j, c, zr, pl.ds(*PARTS[part])]

    def w_arrival(part, slot):
        return w_r.at[part % 2, 0 if part > 1 else slot[0] * 4 + slot[1]]

    def wsend(part, src_slot, dst_slot, device):
        rdma(wview(part, *src_slot), wview(part, *dst_slot), w_s, w_arrival(part, dst_slot), device).start()

    def dcopy(part, slot):
        view = wview(part, *slot)
        return rdma(view, view, d_s, d_r.at[slot[1]], dev(core=1 - c))

    own_a = pltpu.make_async_copy(a_hbm.at[tp * 4 + z, pl.ds(0, NK)], abuf.at[:, :, c, 0], l_sem.at[0])
    ex_a = pltpu.make_async_copy(a_hbm.at[:, NK], ea, l_sem.at[3])
    own_w = pltpu.make_async_copy(w_hbm, wbuf.at[0, c, 0], l_sem.at[1])
    own_r = pltpu.make_async_copy(r_hbm, rbuf, l_sem.at[2])
    own_w.start()
    ex_a.start()
    own_a.start()
    own_r.start()

    barrier = pltpu.get_barrier_semaphore()
    peers = [dev(dx=d, core=cd) for d in AROUND for cd in CORES] + [dev(core=1 - c)]
    peers += [dev(dy=1), dev(dy=3), dev(dz=1), dev(dz=2), dev(dz=3)]
    for peer in peers:
        pl.semaphore_signal(barrier, inc=1, device_id=peer, device_id_type=MESH)
    pl.semaphore_wait(barrier, len(peers))

    def cross_start(k):
        for d in AROUND:
            for cd in CORES:
                cross(k, d, cd).start()

    def bcast_start(k):
        await_bytes(abuf.at[k, y, :, pl.ds(1, 3)], a_r.at[k])
        for i in CORES:
            bcast(k, i, 0).start()
            bcast(k, 1 - i, 1).start()

    def forward_start(k):
        for back in CORES:
            bcast(k, back, back).wait_recv()
            forward(k, back).start()

    def take(part, j, zr):
        await_bytes(wview(part, j, zr), w_arrival(part, (j, zr)))
        dcopy(part, (j, zr)).start()

    def relay_x(part, j, zr):
        take(part, j, zr)
        wsend(part, (j, zr), (2, zr), dev(dx=4 - j))

    def relay_z(j, zr):
        take(1, j, zr)
        wsend(1, (j, zr), (j, 2), dev(dz=4 - zr))

    def both_x(part, zr):
        wsend(part, (0, zr), (3, zr), dev(dx=1))
        wsend(part, (0, zr), (1, zr), dev(dx=3))

    def both_z(part, j):
        wsend(part, (j, 0), (j, 3), dev(dz=1))
        wsend(part, (j, 0), (j, 1), dev(dz=3))

    partner_a = rdma(a_hbm.at[(tp + 1 - 2 * c) * 4 + z, pl.ds(0, NK)], abuf.at[:, :, c, 0],
                     p_s, p_r, dev(core=1 - c))
    own_w.wait()
    wsend(0, (0, 0), (0, 3), dev(dz=1))
    wsend(0, (0, 0), (0, 1), dev(dz=3))
    cross_start(0)
    both_z(1, 0)
    both_x(1, 0)
    wsend(0, (0, 0), (0, 2), dev(dz=2))
    cross_start(1)
    partner_a.start()
    dcopy(0, (0, 0)).start()
    dcopy(1, (0, 0)).start()

    ex_a.wait()

    def ex_copy(d, cd):
        owner = ((x + d) % 4) * 2 + cd
        return rdma(eout.at[owner], ein.at[tp], e_s, e_r, dev(dx=d, core=cd))

    def ex_product(i, carry):
        lhs = ea[pl.ds(i * 4, 4)].reshape(4 * CR, KB)
        prod = jnp.dot(lhs, wbuf[0, c, 0], preferred_element_type=F32)
        eout[i] = prod.astype(BF16).reshape(4, CR, CB)
        return carry

    lax.fori_loop(0, 8, ex_product, 0)

    take(0, 0, 3)
    take(0, 0, 1)
    wsend(0, (0, 3), (3, 3), dev(dx=1))
    wsend(0, (0, 1), (1, 1), dev(dx=3))
    wsend(0, (0, 1), (3, 1), dev(dx=1))
    wsend(0, (0, 3), (1, 3), dev(dx=3))
    bcast_start(0)
    for j, half in HALVES.items():
        take(1, j, 0)
        wsend(half, (j, 0), (2, 0), dev(dx=4 - j))
        both_z(1, j)
    cross_start(2)
    relay_z(0, 3)
    take(1, 0, 1)
    forward_start(0)
    take(0, 0, 2)
    bcast_start(1)
    relay_x(0, 3, 3)
    relay_x(0, 1, 1)
    both_x(0, 2)
    cross_start(3)
    take(0, 3, 1)
    take(0, 1, 3)
    for half in HALVES.values():
        take(half, 2, 0)
    both_z(1, 2)
    relay_z(1, 1)
    relay_z(3, 3)
    forward_start(1)
    bcast_start(2)
    relay_z(2, 1)
    for slot in ((3, 1), (1, 3), (2, 3)):
        take(1, *slot)
    take(0, 2, 3)
    take(0, 2, 1)
    own_a.wait()
    partner_a.wait_recv()

    def partner_w(zr):
        await_bytes(wbuf.at[:, 1 - c, zr], d_r.at[zr])

    partner_w(1)
    partner_w(3)

    def tile(k, zr, out):
        for j in range(4):
            for cc in CORES:
                lhs = abuf[k, :, cc, j].reshape(CR, KB)
                term = jnp.dot(lhs, wbuf[j, cc, zr], preferred_element_type=F32).astype(BF16).astype(F32)
                if j == 0 and cc == 0:
                    out[...] = term
                else:
                    out[...] += term

    def qsend(g, n):
        view = sq.at[g, t2]
        return rdma(view, view, q_s.at[g // LAST], q_r.at[g], dev(dy=n % 4, dz=n // 4))

    def square_group(g):
        for i in CORES:
            k = 2 * g + i
            if k < NK:
                await_bytes(yin.at[pl.ds(0, 3)], y_r.at[k])
            for q in range(4):
                hid = yin[q * NC + k] + rbuf[q, pl.ds(k * CR, CR), :].astype(F32)
                yin[q * NC + k] = hid
                total = jnp.sum(hid * hid, axis=1, keepdims=True)
                sq[g, t2, pl.ds(i * 4 + q, 1), :] = jnp.broadcast_to(total, (CR, 128)).T[0:1, :]
        for n in range(1, 16 if g == LAST else 4):
            qsend(g, n).start()

    def zsend(g, dz):
        view = sz.at[g, z]
        return rdma(view, view, q_s.at[0], z_r.at[g], dev(dz=dz))

    def sum_y(g):
        await_bytes(sq.at[g, pl.ds(0, 3)], q_r.at[g])
        sz[g, z] = jnp.sum(sq[g, pl.ds(z * 4, 4)], axis=0)
        for dz in AROUND:
            zsend(g, dz).start()

    def norm_group(g):
        partial = sq if g == LAST else sz
        await_bytes(partial.at[g, pl.ds(0, 15 if g == LAST else 3)], (q_r if g == LAST else z_r).at[g])
        inv_ref[g] = lax.rsqrt(jnp.sum(partial[g], axis=0) * (1.0 / 4096) + EPS_NORM)

    def step(k, carry):
        await_bytes(abuf.at[k, pl.ds(0, 2), :, pl.ds(1, 3)], f_r.at[k])
        for zr in (1, 3):
            tile(k, zr, yout.at[k, zr - 1])
            ysend(k, zr).start()

        @pl.when(k == 0)
        def _():
            relay_x(0, 3, 2)
            for n in range(4, NK):
                cross_start(n)
            both_x(0, 0)
            forward_start(2)

        @pl.when(k == 1)
        def _():
            bcast_start(3)

        @pl.when(k == 2)
        def _():
            take(0, 1, 2)
            for j in range(4):
                take(1, j, 2)
            take(0, 2, 2)
            partner_w(2)
            bcast_start(4)

        def far(i, carry):
            tile(i, 2, yout.at[i, 1])
            ysend(i, 2).start()
            return carry

        lax.fori_loop(jnp.where(k == 2, 0, k), jnp.where(k < 2, 0, k + 1), far, 0)

        @pl.when(k == 2)
        def _():
            ex_copy(0, 1 - c).start()
            for d in AROUND:
                ex_copy(d, 0).start()
            forward_start(3)
            bcast_start(5)
            forward_start(4)

        @pl.when(k == 3)
        def _():
            relay_x(0, 3, 0)
            take(0, 1, 0)
            for d in AROUND:
                ex_copy(d, 1).start()
            bcast_start(6)
            forward_start(5)

        @pl.when(k == 4)
        def _():
            forward_start(6)

        return carry

    own_r.wait()
    lax.fori_loop(0, NK, step, 0)
    take(0, 2, 0)
    partner_w(0)

    def near(i, carry):
        tile(i, 0, yin.at[z * NC + i])
        return carry

    lax.fori_loop(0, NK, near, 0)

    def ex_sum(q, carry):
        total = eout[tp, q].astype(F32)
        for d in range(1, 8):
            total += ein[(tp + d) % 8, q].astype(F32)
        yin[q * NC + NK] = total
        return carry

    for g in range(LAST):
        square_group(g)
    await_bytes(ein.at[pl.ds(0, 7)], e_r)
    lax.fori_loop(0, 4, ex_sum, 0)
    for g in range(LAST):
        sum_y(g)
    square_group(LAST)
    for g in range(LAST + 1):
        norm_group(g)

    partner_a.wait_send()
    await_bytes(abuf.at[:, :, :, pl.ds(1, 3)], a_s)
    await_bytes(yout, y_s)
    await_bytes(yin.at[pl.ds(0, 30)], w_s)
    await_bytes(yin, d_s)
    await_bytes(eout.at[pl.ds(0, 7)], e_s)
    await_bytes(sq.at[pl.ds(0, LAST), pl.ds(0, 6)], q_s.at[0])
    await_bytes(sq.at[0, pl.ds(0, 15)], q_s.at[1])


def norm_kernel(yin, inv_ref, g_ref, h_hbm, n_hbm, hbuf, nbuf, sem):
    def out_copy(k, which):
        rows = pl.ds(k * CR, CR)
        buf, dst = ((hbuf, h_hbm), (nbuf, n_hbm))[which]
        return pltpu.make_async_copy(buf.at[:, rows], dst.at[:, rows], sem.at[which])

    def chunk(k, carry):
        rows = pl.ds(k * CR, CR)
        for q in range(4):
            inv = inv_ref[k // 2, pl.ds((k % 2) * 4 + q, 1), :]
            scale = jnp.broadcast_to(inv, (128, CR)).T
            hid = yin[q * NC + k]
            hbuf[q, rows, :] = hid.astype(BF16)
            for half in CORES:
                cols = slice(half * 128, half * 128 + 128)
                nbuf[q, rows, cols] = (hid[:, cols] * scale * g_ref[:, cols]).astype(BF16)
        out_copy(k, 0).start()
        out_copy(k, 1).start()
        return carry

    lax.fori_loop(0, NC, chunk, 0)

    for which, buf in enumerate((hbuf, nbuf)):
        pltpu.make_async_copy(buf, buf, sem.at[which]).wait()


def solution(mesh):
    def local_step(attn_blk, w_blk, res_blk, gain_blk):
        any_spec = pl.BlockSpec(memory_space=pl.ANY)
        out = jax.ShapeDtypeStruct((4, NC * CR, CB), BF16)
        vmem_spec = pl.BlockSpec(memory_space=pltpu.VMEM)
        dma = pltpu.SemaphoreType.DMA
        hidden, inv = pl.pallas_call(
            kernel,
            out_shape=(pltpu.VMEM((4 * NC, CR, CB), F32), pltpu.VMEM((NC // 2, 8, 128), F32)),
            in_specs=[any_spec, any_spec, any_spec],
            out_specs=(vmem_spec, vmem_spec),
            scratch_shapes=[
                pltpu.VMEM((NK, 4, 2, 4, SUB, KB), BF16),
                pltpu.VMEM((4, 2, 4, KB, CB), BF16),
                pltpu.VMEM((NK, 3, CR, CB), F32),
                pltpu.VMEM((4, NC * CR, CB), BF16),
                pltpu.VMEM((NC // 2, 16, 8, 128), F32),
                pltpu.VMEM((NC // 2, 4, 8, 128), F32),
                pltpu.VMEM((32, 4, SUB, KB), BF16),
                pltpu.VMEM((8, 4, CR, CB), BF16),
                pltpu.VMEM((8, 4, CR, CB), BF16),
                dma((4,)),
                dma, dma((NK,)), dma, dma, dma((NK, 2)), dma((NK,)),
                dma, dma((2, 16)), dma, dma((4,)), dma, dma((NK,)),
                dma((2,)), dma((LAST + 1,)), dma, dma, dma((LAST,)),
            ],
            compiler_params=pltpu.CompilerParams(
                collective_id=0, has_side_effects=True, vmem_limit_bytes=50 * 1024 * 1024),
        )(attn_blk.reshape(8 * 4, NC, 4, SUB, KB), w_blk, res_blk.reshape(4, NC * CR, CB))
        h, n = pl.pallas_call(
            norm_kernel,
            out_shape=(out, out),
            in_specs=[vmem_spec] * 3,
            out_specs=(any_spec, any_spec),
            scratch_shapes=[pltpu.VMEM((4, NC * CR, CB), BF16)] * 2 + [dma((2,))],
            compiler_params=pltpu.CompilerParams(vmem_limit_bytes=12 * 1024 * 1024),
        )(hidden, inv, gain_blk.reshape(1, CB))
        return h.reshape(4 * NC * CR, CB), n.reshape(4 * NC * CR, CB)

    row_spec = P(("dp", "tp"), "tp2")
    return jax.shard_map(local_step, mesh=mesh, in_specs=(P("dp", "tp"), P("tp", "tp2"), row_spec, P("tp2")),
                         out_specs=(row_spec, row_spec), check_vma=False)
```

time: 95.3 us -> 86.9 us (0.912)
  Pallas kernels: 94.4 us -> 85.8 us
    pallas_call x1, Pallas kernels: 92.2 us -> 83.7 us  [local_step(): pl.pallas_call(kernel, out_shape=(pltpu.VMEM((4 * NC, CR, CB), F32), pltp...]
where the time goes in v3:
time: 86.9 us; the launch traced here: 86.5 us
  Pallas kernels  85.8 us (99%)
    pallas_call x1, Pallas kernels, local_step(): pl.pallas_call(kernel, out_shape=(pltpu.VMEM((4 * NC, CR, CB), F32), pltp...  83.7 us
    pallas_call x1, Pallas kernels, local_step(): pl.pallas_call(norm_kernel, out_shape=(out, out), in_specs=[vmem_spec] *...  2.08 us

profile of v3, /device:TPU:0, one launch (start us, length us, event | category | flops | bytes accessed | tf_op | source)
XLA Modules:
  0.0 86.5 jit_solution(5404539248574604258)
XLA Ops:
  0.6 0.0 copy-start
  0.6 83.7 %shard_map.59 = (f32[32,128,256]{2,1,0:T(8,128)S(1)}, f32[4,8,128]{2,1,0:T(8,128)S(1)}) custom-call(bf16[32,8,4,32,512]{4,3,2,1,0:T(8,128)(2,1)} %bitcast.6, bf16[512,256]{1,0:T(8,128)(2,1)} %w_hbm.1, bf16[4,1024,256]{2,1,0:T(8,128)(2,1)} %bitcast.7), custom_call_target="tpu_custom_call" | custom-call | tf_op jit(solution)/shard_map/pallas_call | solution.py:365
  84.4 0.0 copy-done
  84.4 2.1 %shard_map.60 = (bf16[4,1024,256]{2,1,0:T(8,128)(2,1)}, bf16[4,1024,256]{2,1,0:T(8,128)(2,1)}) custom-call(f32[32,128,256]{2,1,0:T(8,128)S(1)} %get-tuple-element.6.yin, f32[4,8,128]{2,1,0:T(8,128)S(1)} %get-tuple-element.7.inv_ref, f32[1,256]{1,0:T(1,128)S(1)} %bitcast.5), custom_call_target="tpu_custom_call" | custom-call | tf_op jit(solution)/shard_map/pallas_call | solution.py:388
Async XLA Ops:
  0.6 83.7 %copy-start = (f32[256]{0:T(256)S(1)}, f32[256]{0:T(256)}, u32[]{:S(2)}) copy-start(f32[256]{0:T(256)} %param.7) | copy-start | bytes 3076

commit v4 on v3

--- a/solution.py
+++ b/solution.py
@@ -18,13 +18,13 @@
 SUB = 32
 KB = 512
 CB = 256
-PARTS = ((0, 256), (256, 256), (256, 128), (384, 128))
-HALVES = {3: 2, 1: 3}
-
-
-def kernel(a_hbm, w_hbm, r_hbm, yin, inv_ref,
+PARTS = ((0, 256), (256, 256), (0, 128), (128, 128), (256, 128), (384, 128))
+SIDES = ((3, 0), (1, 1))
+
+
+def kernel(a_hbm, w_hbm, r_hbm, yin, hbuf, inv_ref,
            abuf, wbuf, yout, rbuf, sq, sz, ea, eout, ein,
-           l_sem, a_s, a_r, p_s, p_r, b_r, f_r, w_s, w_r, d_s, d_r, y_s, y_r, q_s, q_r, e_s, e_r, z_r):
+           l_sem, a_s, a_r, p_s, p_r, b_r, f_r, w_s, w_r, d_s, d_r, y_s, y_r, q_s, q_r, e_s, e_r, z_r, h_r):
     tp, t2 = lax.axis_index("tp"), lax.axis_index("tp2")
     x, c, z, y = tp // 2, tp % 2, t2 // 4, t2 % 4
 
@@ -59,7 +59,7 @@
         return wbuf.at[j, c, zr, pl.ds(*PARTS[part])]
 
     def w_arrival(part, slot):
-        return w_r.at[part % 2, 0 if part > 1 else slot[0] * 4 + slot[1]]
+        return w_r.at[part, slot[0] * 4 + slot[1]] if part < 2 else h_r.at[part - 2, slot[1]]
 
     def wsend(part, src_slot, dst_slot, device):
         rdma(wview(part, *src_slot), wview(part, *dst_slot), w_s, w_arrival(part, dst_slot), device).start()
@@ -107,6 +107,13 @@
     def relay_x(part, j, zr):
         take(part, j, zr)
         wsend(part, (j, zr), (2, zr), dev(dx=4 - j))
+
+    def pass_half(part, j, zr):
+        wsend(2 + 2 * part + dict(SIDES)[j], (j, zr), (2, zr), dev(dx=4 - j))
+
+    def take_halves(part, zr):
+        for half in CORES:
+            take(2 + 2 * part + half, 2, zr)
 
     def relay_z(j, zr):
         take(1, j, zr)
@@ -155,9 +162,9 @@
     wsend(0, (0, 1), (3, 1), dev(dx=1))
     wsend(0, (0, 3), (1, 3), dev(dx=3))
     bcast_start(0)
-    for j, half in HALVES.items():
+    for j, half in SIDES:
         take(1, j, 0)
-        wsend(half, (j, 0), (2, 0), dev(dx=4 - j))
+        pass_half(1, j, 0)
         both_z(1, j)
     cross_start(2)
     relay_z(0, 3)
@@ -171,8 +178,7 @@
     cross_start(3)
     take(0, 3, 1)
     take(0, 1, 3)
-    for half in HALVES.values():
-        take(half, 2, 0)
+    take_halves(1, 0)
     both_z(1, 2)
     relay_z(1, 1)
     relay_z(3, 3)
@@ -214,6 +220,7 @@
             for q in range(4):
                 hid = yin[q * NC + k] + rbuf[q, pl.ds(k * CR, CR), :].astype(F32)
                 yin[q * NC + k] = hid
+                hbuf[q, pl.ds(k * CR, CR), :] = hid.astype(BF16)
                 total = jnp.sum(hid * hid, axis=1, keepdims=True)
                 sq[g, t2, pl.ds(i * 4 + q, 1), :] = jnp.broadcast_to(total, (CR, 128)).T[0:1, :]
         for n in range(1, 16 if g == LAST else 4):
@@ -242,7 +249,9 @@
 
         @pl.when(k == 0)
         def _():
-            relay_x(0, 3, 2)
+            for j, half in SIDES:
+                take(0, j, 2)
+                pass_half(0, j, 2)
             for n in range(4, NK):
                 cross_start(n)
             both_x(0, 0)
@@ -251,15 +260,13 @@
         @pl.when(k == 1)
         def _():
             bcast_start(3)
-
-        @pl.when(k == 2)
-        def _():
-            take(0, 1, 2)
             for j in range(4):
                 take(1, j, 2)
-            take(0, 2, 2)
+            take_halves(0, 2)
+
+        @pl.when(k == 2)
+        def _():
             partner_w(2)
-            bcast_start(4)
 
         def far(i, carry):
             tile(i, 2, yout.at[i, 1])
@@ -268,33 +275,36 @@
 
         lax.fori_loop(jnp.where(k == 2, 0, k), jnp.where(k < 2, 0, k + 1), far, 0)
 
+        @pl.when((k >= 2) & (k < NK - 1))
+        def _():
+            forward_start(k + 1)
+
+        @pl.when((k >= 2) & (k < NK - 2))
+        def _():
+            bcast_start(k + 2)
+
         @pl.when(k == 2)
         def _():
             ex_copy(0, 1 - c).start()
             for d in AROUND:
                 ex_copy(d, 0).start()
-            forward_start(3)
-            bcast_start(5)
-            forward_start(4)
 
         @pl.when(k == 3)
         def _():
-            relay_x(0, 3, 0)
-            take(0, 1, 0)
+            for j, half in SIDES:
+                take(0, j, 0)
+                pass_half(0, j, 0)
             for d in AROUND:
                 ex_copy(d, 1).start()
-            bcast_start(6)
-            forward_start(5)
-
-        @pl.when(k == 4)
-        def _():
-            forward_start(6)
+
+        @pl.when(k == 5)
+        def _():
+            take_halves(0, 0)
 
         return carry
 
     own_r.wait()
     lax.fori_loop(0, NK, step, 0)
-    take(0, 2, 0)
     partner_w(0)
 
     def near(i, carry):
@@ -312,10 +322,11 @@
 
     for g in range(LAST):
         square_group(g)
+    sum_y(0)
+    sum_y(1)
     await_bytes(ein.at[pl.ds(0, 7)], e_r)
     lax.fori_loop(0, 4, ex_sum, 0)
-    for g in range(LAST):
-        sum_y(g)
+    sum_y(2)
     square_group(LAST)
     for g in range(LAST + 1):
         norm_group(g)
@@ -330,30 +341,24 @@
     await_bytes(sq.at[0, pl.ds(0, 15)], q_s.at[1])
 
 
-def norm_kernel(yin, inv_ref, g_ref, h_hbm, n_hbm, hbuf, nbuf, sem):
-    def out_copy(k, which):
-        rows = pl.ds(k * CR, CR)
-        buf, dst = ((hbuf, h_hbm), (nbuf, n_hbm))[which]
-        return pltpu.make_async_copy(buf.at[:, rows], dst.at[:, rows], sem.at[which])
+def norm_kernel(yin, hbuf, inv_ref, g_ref, h_hbm, n_hbm, nbuf, sem):
+    h_copy = pltpu.make_async_copy(hbuf, h_hbm, sem.at[0])
+    h_copy.start()
 
     def chunk(k, carry):
         rows = pl.ds(k * CR, CR)
         for q in range(4):
             inv = inv_ref[k // 2, pl.ds((k % 2) * 4 + q, 1), :]
             scale = jnp.broadcast_to(inv, (128, CR)).T
-            hid = yin[q * NC + k]
-            hbuf[q, rows, :] = hid.astype(BF16)
             for half in CORES:
-                cols = slice(half * 128, half * 128 + 128)
-                nbuf[q, rows, cols] = (hid[:, cols] * scale * g_ref[:, cols]).astype(BF16)
-        out_copy(k, 0).start()
-        out_copy(k, 1).start()
+                cols = pl.ds(half * 128, 128)
+                nbuf[q, rows, cols] = (yin[q * NC + k, :, cols] * scale * g_ref[:, cols]).astype(BF16)
+        pltpu.make_async_copy(nbuf.at[:, rows], n_hbm.at[:, rows], sem.at[1]).start()
         return carry
 
     lax.fori_loop(0, NC, chunk, 0)
-
-    for which, buf in enumerate((hbuf, nbuf)):
-        pltpu.make_async_copy(buf, buf, sem.at[which]).wait()
+    h_copy.wait()
+    pltpu.make_async_copy(nbuf, n_hbm, sem.at[1]).wait()
 
 
 def solution(mesh):
@@ -362,11 +367,12 @@
         out = jax.ShapeDtypeStruct((4, NC * CR, CB), BF16)
         vmem_spec = pl.BlockSpec(memory_space=pltpu.VMEM)
         dma = pltpu.SemaphoreType.DMA
-        hidden, inv = pl.pallas_call(
+        hidden, h_bf16, inv = pl.pallas_call(
             kernel,
-            out_shape=(pltpu.VMEM((4 * NC, CR, CB), F32), pltpu.VMEM((NC // 2, 8, 128), F32)),
+            out_shape=(pltpu.VMEM((4 * NC, CR, CB), F32), pltpu.VMEM((4, NC * CR, CB), BF16),
+                       pltpu.VMEM((NC // 2, 8, 128), F32)),
             in_specs=[any_spec, any_spec, any_spec],
-            out_specs=(vmem_spec, vmem_spec),
+            out_specs=(vmem_spec,) * 3,
             scratch_shapes=[
                 pltpu.VMEM((NK, 4, 2, 4, SUB, KB), BF16),
                 pltpu.VMEM((4, 2, 4, KB, CB), BF16),
@@ -380,7 +386,7 @@
                 dma((4,)),
                 dma, dma((NK,)), dma, dma, dma((NK, 2)), dma((NK,)),
                 dma, dma((2, 16)), dma, dma((4,)), dma, dma((NK,)),
-                dma((2,)), dma((LAST + 1,)), dma, dma, dma((LAST,)),
+                dma((2,)), dma((LAST + 1,)), dma, dma, dma((LAST,)), dma((4, 4)),
             ],
             compiler_params=pltpu.CompilerParams(
                 collective_id=0, has_side_effects=True, vmem_limit_bytes=50 * 1024 * 1024),
@@ -388,11 +394,11 @@
         h, n = pl.pallas_call(
             norm_kernel,
             out_shape=(out, out),
-            in_specs=[vmem_spec] * 3,
+            in_specs=[vmem_spec] * 4,
             out_specs=(any_spec, any_spec),
-            scratch_shapes=[pltpu.VMEM((4, NC * CR, CB), BF16)] * 2 + [dma((2,))],
+            scratch_shapes=[pltpu.VMEM((4, NC * CR, CB), BF16), dma((2,))],
             compiler_params=pltpu.CompilerParams(vmem_limit_bytes=12 * 1024 * 1024),
-        )(hidden, inv, gain_blk.reshape(1, CB))
+        )(hidden, h_bf16, inv, gain_blk.reshape(1, CB))
         return h.reshape(4 * NC * CR, CB), n.reshape(4 * NC * CR, CB)
 
     row_spec = P(("dp", "tp"), "tp2")

time: 86.9 us -> 84 us (0.967)
  Pallas kernels: 85.8 us -> 83.3 us
    pallas_call x1, Pallas kernels: 83.7 us -> 81.3 us  [local_step(): pl.pallas_call(kernel, out_shape=(pltpu.VMEM((4 * NC, CR, CB), F32), pltp...]
where the time goes in v4:
time: 84 us; the launch traced here: 83.9 us
  Pallas kernels  83.3 us (99%)
    pallas_call x1, Pallas kernels, local_step(): pl.pallas_call(kernel, out_shape=(pltpu.VMEM((4 * NC, CR, CB), F32), pltp...  81.3 us
    pallas_call x1, Pallas kernels, local_step(): pl.pallas_call(norm_kernel, out_shape=(out, out), in_specs=[vmem_spec] *...  2.01 us

profile of v4, /device:TPU:0, one launch (start us, length us, event | category | flops | bytes accessed | tf_op | source)
XLA Modules:
  0.0 83.9 jit_solution(17908551512487154728)
XLA Ops:
  0.6 0.0 copy-start
  0.6 81.3 %shard_map.59 = (f32[32,128,256]{2,1,0:T(8,128)S(1)}, bf16[4,1024,256]{2,1,0:T(8,128)(2,1)S(1)}, f32[4,8,128]{2,1,0:T(8,128)S(1)}) custom-call(bf16[32,8,4,32,512]{4,3,2,1,0:T(8,128)(2,1)} %bitcast.6, bf16[512,256]{1,0:T(8,128)(2,1)} %w_hbm.1, bf16[4,1024,256]{2,1,0:T(8,128)(2,1)} %bitcast.7), custom_call_target="tpu_custom_call" | custom-call | tf_op jit(solution)/shard_map/pallas_call | solution.py:370
  81.9 0.0 copy-done
  81.9 2.0 %shard_map.60 = (bf16[4,1024,256]{2,1,0:T(8,128)(2,1)}, bf16[4,1024,256]{2,1,0:T(8,128)(2,1)}) custom-call(f32[32,128,256]{2,1,0:T(8,128)S(1)} %get-tuple-element.7.yin, bf16[4,1024,256]{2,1,0:T(8,128)(2,1)S(1)} %get-tuple-element.8.hbuf, f32[4,8,128]{2,1,0:T(8,128)S(1)} %get-tuple-element.9.inv_ref, f32[1,256]{1,0:T(1,128)S(1)} %bitcast.5), custom_call_target="tpu_custom_call" | custom-call | tf_op jit(solution)/shard_map/pallas_call | solution.py:394
Async XLA Ops:
  0.6 81.3 %copy-start = (f32[256]{0:T(256)S(1)}, f32[256]{0:T(256)}, u32[]{:S(2)}) copy-start(f32[256]{0:T(256)} %param.7) | copy-start | bytes 3076

commit v5 on v4

--- a/solution.py
+++ b/solution.py
@@ -59,7 +59,7 @@
         return wbuf.at[j, c, zr, pl.ds(*PARTS[part])]
 
     def w_arrival(part, slot):
-        return w_r.at[part, slot[0] * 4 + slot[1]] if part < 2 else h_r.at[part - 2, slot[1]]
+        return w_r.at[part, slot[0] * 4 + slot[1]] if part < 2 else h_r.at[part - 2, slot[1] // 2]
 
     def wsend(part, src_slot, dst_slot, device):
         rdma(wview(part, *src_slot), wview(part, *dst_slot), w_s, w_arrival(part, dst_slot), device).start()
@@ -132,9 +132,9 @@
     own_w.wait()
     wsend(0, (0, 0), (0, 3), dev(dz=1))
     wsend(0, (0, 0), (0, 1), dev(dz=3))
+    both_x(1, 0)
     cross_start(0)
     both_z(1, 0)
-    both_x(1, 0)
     wsend(0, (0, 0), (0, 2), dev(dz=2))
     cross_start(1)
     partner_a.start()
@@ -213,7 +213,7 @@
         return rdma(view, view, q_s.at[g // LAST], q_r.at[g], dev(dy=n % 4, dz=n // 4))
 
     def square_group(g):
-        for i in CORES:
+        for i in (1, 0) if g == LAST else CORES:
             k = 2 * g + i
             if k < NK:
                 await_bytes(yin.at[pl.ds(0, 3)], y_r.at[k])
@@ -252,14 +252,15 @@
             for j, half in SIDES:
                 take(0, j, 2)
                 pass_half(0, j, 2)
-            for n in range(4, NK):
+            cross_start(4)
+            forward_start(2)
+
+        @pl.when(k == 1)
+        def _():
+            bcast_start(3)
+            for n in range(5, NK):
                 cross_start(n)
             both_x(0, 0)
-            forward_start(2)
-
-        @pl.when(k == 1)
-        def _():
-            bcast_start(3)
             for j in range(4):
                 take(1, j, 2)
             take_halves(0, 2)
@@ -386,7 +387,7 @@
                 dma((4,)),
                 dma, dma((NK,)), dma, dma, dma((NK, 2)), dma((NK,)),
                 dma, dma((2, 16)), dma, dma((4,)), dma, dma((NK,)),
-                dma((2,)), dma((LAST + 1,)), dma, dma, dma((LAST,)), dma((4, 4)),
+                dma((2,)), dma((LAST + 1,)), dma, dma, dma((LAST,)), dma((4, 2)),
             ],
             compiler_params=pltpu.CompilerParams(
                 collective_id=0, has_side_effects=True, vmem_limit_bytes=50 * 1024 * 1024),

time: 84 us -> 84 us (level)
  no operation moved by 1% of the time
where the time goes in v5:
time: 84 us; the launch traced here: 83.8 us
  Pallas kernels  83.2 us (99%)
    pallas_call x1, Pallas kernels, local_step(): pl.pallas_call(kernel, out_shape=(pltpu.VMEM((4 * NC, CR, CB), F32), pltp...  81.2 us
    pallas_call x1, Pallas kernels, local_step(): pl.pallas_call(norm_kernel, out_shape=(out, out), in_specs=[vmem_spec] *...  2.01 us

profile of v5, /device:TPU:0, one launch (start us, length us, event | category | flops | bytes accessed | tf_op | source)
XLA Modules:
  0.0 83.8 jit_solution(2682913178409750623)
XLA Ops:
  0.6 0.0 copy-start
  0.6 81.2 %shard_map.59 = (f32[32,128,256]{2,1,0:T(8,128)S(1)}, bf16[4,1024,256]{2,1,0:T(8,128)(2,1)S(1)}, f32[4,8,128]{2,1,0:T(8,128)S(1)}) custom-call(bf16[32,8,4,32,512]{4,3,2,1,0:T(8,128)(2,1)} %bitcast.6, bf16[512,256]{1,0:T(8,128)(2,1)} %w_hbm.1, bf16[4,1024,256]{2,1,0:T(8,128)(2,1)} %bitcast.7), custom_call_target="tpu_custom_call" | custom-call | tf_op jit(solution)/shard_map/pallas_call | solution.py:371
  81.8 0.0 copy-done
  81.8 2.0 %shard_map.60 = (bf16[4,1024,256]{2,1,0:T(8,128)(2,1)}, bf16[4,1024,256]{2,1,0:T(8,128)(2,1)}) custom-call(f32[32,128,256]{2,1,0:T(8,128)S(1)} %get-tuple-element.7.yin, bf16[4,1024,256]{2,1,0:T(8,128)(2,1)S(1)} %get-tuple-element.8.hbuf, f32[4,8,128]{2,1,0:T(8,128)S(1)} %get-tuple-element.9.inv_ref, f32[1,256]{1,0:T(1,128)S(1)} %bitcast.5), custom_call_target="tpu_custom_call" | custom-call | tf_op jit(solution)/shard_map/pallas_call | solution.py:395
Async XLA Ops:
  0.6 81.2 %copy-start = (f32[256]{0:T(256)S(1)}, f32[256]{0:T(256)}, u32[]{:S(2)}) copy-start(f32[256]{0:T(256)} %param.7) | copy-start | bytes 3076

commit v6 on v5

--- a/solution.py
+++ b/solution.py
@@ -9,6 +9,7 @@
 MESH = pl.DeviceIdType.MESH
 AROUND = (1, 3, 2)
 CORES = (0, 1)
+FAR_FIRST = sorted(range(1, 16), key=lambda n: (n % 4 != 2) + (n % 4 == 0) + (n // 4 != 2) + (n // 4 == 0))
 BF16, F32 = jnp.bfloat16, jnp.float32
 
 NC = 8
@@ -223,7 +224,7 @@
                 hbuf[q, pl.ds(k * CR, CR), :] = hid.astype(BF16)
                 total = jnp.sum(hid * hid, axis=1, keepdims=True)
                 sq[g, t2, pl.ds(i * 4 + q, 1), :] = jnp.broadcast_to(total, (CR, 128)).T[0:1, :]
-        for n in range(1, 16 if g == LAST else 4):
+        for n in FAR_FIRST if g == LAST else AROUND:
             qsend(g, n).start()
 
     def zsend(g, dz):

time: 84 us -> 83.7 us (level)
  no operation moved by 1% of the time
where the time goes in v6:
time: 83.7 us; the launch traced here: 83.6 us
  Pallas kernels  83 us (99%)
    pallas_call x1, Pallas kernels, local_step(): pl.pallas_call(kernel, out_shape=(pltpu.VMEM((4 * NC, CR, CB), F32), pltp...  80.9 us
    pallas_call x1, Pallas kernels, local_step(): pl.pallas_call(norm_kernel, out_shape=(out, out), in_specs=[vmem_spec] *...  2.01 us

profile of v6, /device:TPU:0, one launch (start us, length us, event | category | flops | bytes accessed | tf_op | source)
XLA Modules:
  0.0 83.6 jit_solution(15848768385606534498)
XLA Ops:
  0.6 0.0 copy-start
  0.6 80.9 %shard_map.59 = (f32[32,128,256]{2,1,0:T(8,128)S(1)}, bf16[4,1024,256]{2,1,0:T(8,128)(2,1)S(1)}, f32[4,8,128]{2,1,0:T(8,128)S(1)}) custom-call(bf16[32,8,4,32,512]{4,3,2,1,0:T(8,128)(2,1)} %bitcast.6, bf16[512,256]{1,0:T(8,128)(2,1)} %w_hbm.1, bf16[4,1024,256]{2,1,0:T(8,128)(2,1)} %bitcast.7), custom_call_target="tpu_custom_call" | custom-call | tf_op jit(solution)/shard_map/pallas_call | solution.py:372
  81.6 0.0 copy-done
  81.6 2.0 %shard_map.60 = (bf16[4,1024,256]{2,1,0:T(8,128)(2,1)}, bf16[4,1024,256]{2,1,0:T(8,128)(2,1)}) custom-call(f32[32,128,256]{2,1,0:T(8,128)S(1)} %get-tuple-element.7.yin, bf16[4,1024,256]{2,1,0:T(8,128)(2,1)S(1)} %get-tuple-element.8.hbuf, f32[4,8,128]{2,1,0:T(8,128)S(1)} %get-tuple-element.9.inv_ref, f32[1,256]{1,0:T(1,128)S(1)} %bitcast.5), custom_call_target="tpu_custom_call" | custom-call | tf_op jit(solution)/shard_map/pallas_call | solution.py:396
Async XLA Ops:
  0.6 81.0 %copy-start = (f32[256]{0:T(256)S(1)}, f32[256]{0:T(256)}, u32[]{:S(2)}) copy-start(f32[256]{0:T(256)} %param.7) | copy-start | bytes 3076

commit v7 on v6

--- a/solution.py
+++ b/solution.py
@@ -25,7 +25,7 @@
 
 def kernel(a_hbm, w_hbm, r_hbm, yin, hbuf, inv_ref,
            abuf, wbuf, yout, rbuf, sq, sz, ea, eout, ein,
-           l_sem, a_s, a_r, p_s, p_r, b_r, f_r, w_s, w_r, d_s, d_r, y_s, y_r, q_s, q_r, e_s, e_r, z_r, h_r):
+           l_sem, a_s, a_r, p_s, p_r, b_r, f_r, w_s, w_r, d_s, d_r, y_s, y_r, q_s, q_r, e_s, e_r, z_r):
     tp, t2 = lax.axis_index("tp"), lax.axis_index("tp2")
     x, c, z, y = tp // 2, tp % 2, t2 // 4, t2 % 4
 
@@ -59,8 +59,14 @@
     def wview(part, j, zr):
         return wbuf.at[j, c, zr, pl.ds(*PARTS[part])]
 
+    w_index = {}
+
     def w_arrival(part, slot):
-        return w_r.at[part, slot[0] * 4 + slot[1]] if part < 2 else h_r.at[part - 2, slot[1] // 2]
+        if part > 1:
+            key = (part // 2, slot[1])
+        else:
+            key = (part, "far") if part == 1 and slot[1] == 2 else (part, slot)
+        return w_r.at[w_index.setdefault(key, len(w_index))]
 
     def wsend(part, src_slot, dst_slot, device):
         rdma(wview(part, *src_slot), wview(part, *dst_slot), w_s, w_arrival(part, dst_slot), device).start()
@@ -113,8 +119,8 @@
         wsend(2 + 2 * part + dict(SIDES)[j], (j, zr), (2, zr), dev(dx=4 - j))
 
     def take_halves(part, zr):
-        for half in CORES:
-            take(2 + 2 * part + half, 2, zr)
+        await_bytes(wview(part, 2, zr), w_arrival(2 + 2 * part, (2, zr)))
+        dcopy(part, (2, zr)).start()
 
     def relay_z(j, zr):
         take(1, j, zr)
@@ -262,8 +268,9 @@
             for n in range(5, NK):
                 cross_start(n)
             both_x(0, 0)
+            await_bytes(wbuf.at[:, c, 2, pl.ds(*PARTS[1])], w_arrival(1, (0, 2)))
             for j in range(4):
-                take(1, j, 2)
+                dcopy(1, (j, 2)).start()
             take_halves(0, 2)
 
         @pl.when(k == 2)
@@ -387,8 +394,8 @@
                 pltpu.VMEM((8, 4, CR, CB), BF16),
                 dma((4,)),
                 dma, dma((NK,)), dma, dma, dma((NK, 2)), dma((NK,)),
-                dma, dma((2, 16)), dma, dma((4,)), dma, dma((NK,)),
-                dma((2,)), dma((LAST + 1,)), dma, dma, dma((LAST,)), dma((4, 2)),
+                dma, dma((27,)), dma, dma((4,)), dma, dma((NK,)),
+                dma((2,)), dma((LAST + 1,)), dma, dma, dma((LAST,)),
             ],
             compiler_params=pltpu.CompilerParams(
                 collective_id=0, has_side_effects=True, vmem_limit_bytes=50 * 1024 * 1024),

time: 83.7 us -> 83.6 us (level)
  no operation moved by 1% of the time
where the time goes in v7:
time: 83.6 us; the launch traced here: 83.5 us
  Pallas kernels  82.8 us (99%)
    pallas_call x1, Pallas kernels, local_step(): pl.pallas_call(kernel, out_shape=(pltpu.VMEM((4 * NC, CR, CB), F32), pltp...  80.8 us
    pallas_call x1, Pallas kernels, local_step(): pl.pallas_call(norm_kernel, out_shape=(out, out), in_specs=[vmem_spec] *...  2.01 us

profile of v7, /device:TPU:0, one launch (start us, length us, event | category | flops | bytes accessed | tf_op | source)
XLA Modules:
  0.0 83.5 jit_solution(17857432435770405281)
XLA Ops:
  0.6 0.0 copy-start
  0.6 80.8 %shard_map.59 = (f32[32,128,256]{2,1,0:T(8,128)S(1)}, bf16[4,1024,256]{2,1,0:T(8,128)(2,1)S(1)}, f32[4,8,128]{2,1,0:T(8,128)S(1)}) custom-call(bf16[32,8,4,32,512]{4,3,2,1,0:T(8,128)(2,1)} %bitcast.6, bf16[512,256]{1,0:T(8,128)(2,1)} %w_hbm.1, bf16[4,1024,256]{2,1,0:T(8,128)(2,1)} %bitcast.7), custom_call_target="tpu_custom_call" | custom-call | tf_op jit(solution)/shard_map/pallas_call | solution.py:379
  81.5 0.0 copy-done
  81.5 2.0 %shard_map.60 = (bf16[4,1024,256]{2,1,0:T(8,128)(2,1)}, bf16[4,1024,256]{2,1,0:T(8,128)(2,1)}) custom-call(f32[32,128,256]{2,1,0:T(8,128)S(1)} %get-tuple-element.7.yin, bf16[4,1024,256]{2,1,0:T(8,128)(2,1)S(1)} %get-tuple-element.8.hbuf, f32[4,8,128]{2,1,0:T(8,128)S(1)} %get-tuple-element.9.inv_ref, f32[1,256]{1,0:T(1,128)S(1)} %bitcast.5), custom_call_target="tpu_custom_call" | custom-call | tf_op jit(solution)/shard_map/pallas_call | solution.py:403
Async XLA Ops:
  0.6 80.8 %copy-start = (f32[256]{0:T(256)S(1)}, f32[256]{0:T(256)}, u32[]{:S(2)}) copy-start(f32[256]{0:T(256)} %param.7) | copy-start | bytes 3076
